TPU v7x, 32 devices: a whole 2x2x4 slice. The times are simulated.
32 devices in a mesh: rep: 8 (over y, x, core), tp: 4 (over z).
Axes of the slice: x: 2, y: 2, z: 4, core: 2. Of those that a mesh axis runs over, the one named last changes fastest.
Arguments:
- tokens: bfloat16 [8192, 1280], P(('rep', 'tp')), may hold values from -6 to 6
- view_ids: int32 [32, 4], P('rep'), may hold values from 0 to 31
- time_ids: int32 [32], P('rep'), may hold values from 0 to 999
- camera_table: float32 [32, 1280], replicated, may hold values from -6 to 6
- norm_attn: float32 [2, 1280], replicated, may hold values from 0.1 to 1.9
- norm_ffn: float32 [2, 1280], replicated, may hold values from 0.1 to 1.9
- w_query: bfloat16 [2, 1280, 1280], P(None, ('rep', 'tp')), may hold values from -0.1677051 to 0.1677051
- w_key: bfloat16 [2, 1280, 1280], P(None, ('rep', 'tp')), may hold values from -6.764106 to 6.764106
- w_value: bfloat16 [2, 1280, 1280], P(None, ('rep', 'tp')), may hold values from -0.15625 to 0.15625
- w_out: bfloat16 [2, 1280, 1280], P(None, ('rep', 'tp')), may hold values from -0.15625 to 0.15625
- w_gate: bfloat16 [2, 1280, 5120], P(None, ('rep', 'tp')), may hold values from -0.15625 to 0.15625
- w_up: bfloat16 [2, 1280, 5120], P(None, ('rep', 'tp')), may hold values from -0.15625 to 0.15625
- w_down: bfloat16 [2, 1280, 5120], P(None, ('rep', 'tp')), may hold values from -0.078125 to 0.078125
Outputs:
- denoised: bfloat16 [8192, 1280], P(('rep', 'tp'))
All inputs are finite; a program needn't handle non-finite values.
Results may differ from a plain program's by a relative error of at most 0.035.
Values may be sent and summed in bfloat16 or wider, within the bound.
A program may use at most 128 MiB of HBM per device.

v0:
```python
import math
import jax
import jax.numpy as jnp
from jax import lax
from jax.sharding import PartitionSpec as P

D = 1280
HEADS = 8
VIEWS = 4
HW = 64
LAYERS = 2


def layer_norm(activations, gain_vector):
    average = jnp.mean(activations, axis=-1, keepdims=True)
    centred = activations - average
    spread = jnp.mean(centred * centred, axis=-1, keepdims=True)
    return (centred * lax.rsqrt(spread + 1e-05) * gain_vector).astype(jnp.bfloat16)


def time_code(step_ids, width):
    half_width = width // 2
    frequency = jnp.exp(-math.log(10000.0) * jnp.arange(half_width, dtype=jnp.float32) / half_width)
    angles = step_ids.astype(jnp.float32)[:, None] * frequency[None, :]
    return jnp.concatenate([jnp.cos(angles), jnp.sin(angles)], axis=1)


def conditioning(row_ids, view_ids, time_ids, camera_table):
    set_ids = row_ids // (VIEWS * HW)
    slot_ids = set_ids * VIEWS + row_ids // HW % VIEWS
    flat_views = view_ids.reshape(-1)
    slot_range = jnp.arange(flat_views.shape[0], dtype=jnp.int32)
    pose_ids = jnp.sum(
        jnp.where(slot_ids[:, None] == slot_range[None, :], flat_views[None, :], 0), axis=1
    )
    set_range = jnp.arange(time_ids.shape[0], dtype=jnp.int32)
    step_ids = jnp.sum(
        jnp.where(set_ids[:, None] == set_range[None, :], time_ids[None, :], 0), axis=1
    )
    pose_range = jnp.arange(camera_table.shape[0], dtype=jnp.int32)
    onehot_pose = (pose_ids[:, None] == pose_range[None, :]).astype(jnp.float32)
    camera = jnp.dot(onehot_pose, camera_table, precision=lax.Precision.HIGHEST)
    return camera + time_code(step_ids, camera_table.shape[1])


def reshard(weights):
    owned = (
        lax.all_to_all(weights[0], "tp", split_axis=2, concat_axis=1, tiled=True),
        lax.all_to_all(weights[1], "tp", split_axis=2, concat_axis=1, tiled=True),
        lax.all_to_all(weights[2], "tp", split_axis=2, concat_axis=1, tiled=True),
        lax.all_to_all(weights[3], "tp", split_axis=2, concat_axis=1, tiled=True),
        lax.all_to_all(weights[4], "tp", split_axis=2, concat_axis=1, tiled=True),
        lax.all_to_all(weights[5], "tp", split_axis=2, concat_axis=1, tiled=True),
        lax.all_to_all(weights[6], "tp", split_axis=2, concat_axis=1, tiled=True),
    )
    return (
        lax.all_gather(owned[0], "rep", axis=1, tiled=True),
        lax.all_gather(owned[1], "rep", axis=1, tiled=True),
        lax.all_gather(owned[2], "rep", axis=1, tiled=True),
        lax.all_gather(owned[3], "rep", axis=1, tiled=True),
        lax.all_gather(owned[4], "rep", axis=1, tiled=True),
        lax.all_gather(owned[5], "rep", axis=1, tiled=True),
        lax.all_gather(owned[6], "rep", axis=1, tiled=True),
    )


def attend(packed, width_local, head_size):
    total_rows = packed.shape[0]
    set_count = total_rows // (VIEWS * HW)
    heads_here = width_local // head_size
    shape_heads = (set_count, VIEWS * HW, heads_here, head_size)
    query_rows = packed[:, :width_local].reshape(shape_heads)
    key_rows = packed[:, width_local : 2 * width_local].reshape(shape_heads)
    value_rows = packed[:, 2 * width_local :].reshape(shape_heads)
    scores = jnp.einsum(
        "bqhd,bkhd->bhqk", query_rows, key_rows, preferred_element_type=jnp.float32
    ) * head_size ** (-0.5)
    peak = jnp.max(scores, axis=-1, keepdims=True)
    expons = jnp.exp(scores - peak)
    attn_probs = (expons / jnp.sum(expons, axis=-1, keepdims=True)).astype(jnp.bfloat16)
    mixed_rows = jnp.einsum(
        "bhqk,bkhd->bqhd", attn_probs, value_rows, preferred_element_type=jnp.float32
    )
    return mixed_rows.astype(jnp.bfloat16).reshape(total_rows, width_local)


def out_terms(mixed_rows, weight):
    return lax.dot_general(
        mixed_rows, weight, (((1,), (1,)), ((), ())), preferred_element_type=jnp.float32
    )


def body(
    tokens,
    view_ids,
    time_ids,
    camera_table,
    norm_attn,
    norm_ffn,
    w_query,
    w_key,
    w_value,
    w_out,
    w_gate,
    w_up,
    w_down,
):
    tp_count = lax.axis_size("tp")
    query_w, key_w, value_w, out_w, gate_w, up_w, down_w = reshard(
        (w_query, w_key, w_value, w_out, w_gate, w_up, w_down)
    )
    width_local = query_w.shape[2]
    head_size = D // HEADS
    share_rows = tokens.shape[0]
    group_total = share_rows * tp_count
    first_row = lax.axis_index("tp") * share_rows
    whole_rows = lax.all_gather(tokens, "tp", axis=0, tiled=True)
    row_ids = jnp.arange(group_total, dtype=jnp.int32)
    stream = whole_rows.astype(jnp.float32) + conditioning(
        row_ids, view_ids, time_ids, camera_table
    )

    def total_terms(partial_value):
        return lax.psum(partial_value.astype(jnp.bfloat16), "tp").astype(jnp.float32)

    for layer_index in range(LAYERS):
        query_here = query_w[layer_index]
        key_here = key_w[layer_index]
        value_here = value_w[layer_index]
        gate_here = gate_w[layer_index]
        up_here = up_w[layer_index]
        normed = layer_norm(stream, norm_attn[layer_index])
        packed = jnp.concatenate(
            [
                jnp.dot(normed, query_here, preferred_element_type=jnp.float32).astype(
                    jnp.bfloat16
                ),
                jnp.dot(normed, key_here, preferred_element_type=jnp.float32).astype(jnp.bfloat16),
                jnp.dot(normed, value_here, preferred_element_type=jnp.float32).astype(
                    jnp.bfloat16
                ),
            ],
            axis=1,
        )
        mixed_rows = attend(packed, width_local, head_size)
        stream = stream + total_terms(out_terms(mixed_rows, out_w[layer_index]))
        normed = layer_norm(stream, norm_ffn[layer_index])
        gate_part = jnp.dot(normed, gate_here, preferred_element_type=jnp.float32)
        up_part = jnp.dot(normed, up_here, preferred_element_type=jnp.float32)
        hidden = (jax.nn.gelu(gate_part, approximate=False) * up_part).astype(jnp.bfloat16)
        stream = stream + total_terms(out_terms(hidden, down_w[layer_index]))
    return lax.dynamic_slice_in_dim(stream, first_row, share_rows, 0).astype(jnp.bfloat16)


def solution(mesh):
    return jax.shard_map(
        body,
        mesh=mesh,
        in_specs=(
            P(("rep", "tp"), None),
            P("rep", None),
            P("rep"),
            P(),
            P(),
            P(),
            P(None, ("rep", "tp"), None),
            P(None, ("rep", "tp"), None),
            P(None, ("rep", "tp"), None),
            P(None, ("rep", "tp"), None),
            P(None, ("rep", "tp"), None),
            P(None, ("rep", "tp"), None),
            P(None, ("rep", "tp"), None),
        ),
        out_specs=P(("rep", "tp"), None),
        check_vma=False,
    )
```

profile of v0, /device:TPU:0, one launch (start us, length us, event | category | flops | bytes accessed | tf_op | source)
XLA Modules:
  0.0 892.5 jit_solution(10918619393631502398)
XLA Ops:
  9.8 13.8 %all_to_all.126 = bf16[4,2,12800]{2,1,0:T(2,128)(2,1)S(1)} all-to-all(bf16[4,2,12800]{2,1,0:T(2,128)(2,1)S(1)} %reshape.139), channel_id=1, replica_groups=mesh['rep'=8,'tp'=4] {'tp'}, dimensions={0} | all-to-all | bytes 409600 | tf_op jit(solution)/shard_map/all_to_all | solution.py:48
  27.8 19.7 %all_to_all.127 = bf16[4,2,12800]{2,1,0:T(2,128)(2,1)S(1)} all-to-all(bf16[4,2,12800]{2,1,0:T(2,128)(2,1)S(1)} %reshape.137), channel_id=1, replica_groups=mesh['rep'=8,'tp'=4] {'tp'}, dimensions={0} | all-to-all | bytes 409600 | tf_op jit(solution)/shard_map/all_to_all | solution.py:49
  51.7 14.9 %all_to_all.128 = bf16[4,2,12800]{2,1,0:T(2,128)(2,1)S(1)} all-to-all(bf16[4,2,12800]{2,1,0:T(2,128)(2,1)S(1)} %reshape.141), channel_id=1, replica_groups=mesh['rep'=8,'tp'=4] {'tp'}, dimensions={0} | all-to-all | bytes 409600 | tf_op jit(solution)/shard_map/all_to_all | solution.py:50
  75.7 10.5 %multiply_cosine_fusion = (f32[1024,640]{1,0:T(8,128)S(1)}, f32[1024,640]{1,0:T(8,128)}) fusion(f32[640]{0:T(1024)S(1)} %multiply_exponential_fusion, f32[1024]{0:T(1024)S(1)} %convert_element_type.93), kind=kLoop, calls=%fused_computation.60 | loop fusion | flops 655360 | bytes 5249536 | tf_op jit(solution)/shard_map/cos | solution.py:25
  91.8 5.1 fusion.139
  100.0 4.8 all-gather.13.cloned.1.call-done
  109.7 24.3 %all-gather.15.cloned.1.call-done = bf16[2,1280,320]{2,1,0:T(8,128)(2,1)} async-done(((bf16[2,160,320]{2,1,0:T(8,128)(2,1)}), bf16[2,1280,320]{2,1,0:T(8,128)(2,1)}) %all-gather.15.cloned.1.call-update) | async-done | bytes 1638416 | tf_op jit(solution)/shard_map/all_gather | solution.py:58
  139.5 23.4 %all-gather.11.cloned.1.call-done = bf16[2,1280,320]{2,1,0:T(8,128)(2,1)} async-done(((bf16[2,160,320]{2,1,0:T(8,128)(2,1)}), bf16[2,1280,320]{2,1,0:T(8,128)(2,1)}) %all-gather.11.cloned.1.call-update) | async-done | bytes 1638416 | tf_op jit(solution)/shard_map/all_gather | solution.py:59
  173.8 18.1 %all-gather.17.cloned.1.call-done = bf16[2,1280,320]{2,1,0:T(8,128)(2,1)} async-done(((bf16[2,160,320]{2,1,0:T(8,128)(2,1)}), bf16[2,1280,320]{2,1,0:T(8,128)(2,1)}) %all-gather.17.cloned.1.call-update) | async-done | bytes 1638416 | tf_op jit(solution)/shard_map/all_gather | solution.py:60
  192.0 4.3 convolution_convert_fusion.3
  196.6 4.7 copy.97
  201.3 5.1 reshape.145
  206.4 47.9 %all_to_all.129 = bf16[4,2,51200]{2,1,0:T(2,128)(2,1)} all-to-all(bf16[4,2,51200]{2,1,0:T(2,128)(2,1)} %reshape.145), channel_id=1, replica_groups=mesh['rep'=8,'tp'=4] {'tp'}, dimensions={0} | all-to-all | bytes 1638400 | tf_op jit(solution)/shard_map/all_to_all | solution.py:52
  254.2 5.0 reshape.146
  259.3 4.3 copy.117
  265.8 4.7 copy.100
  270.6 5.1 reshape.147
  275.6 47.5 %all_to_all.130 = bf16[4,2,51200]{2,1,0:T(2,128)(2,1)} all-to-all(bf16[4,2,51200]{2,1,0:T(2,128)(2,1)} %reshape.147), channel_id=1, replica_groups=mesh['rep'=8,'tp'=4] {'tp'}, dimensions={0} | all-to-all | bytes 1638400 | tf_op jit(solution)/shard_map/all_to_all | solution.py:53
  323.2 5.0 reshape.148
  334.7 4.7 copy.103
  339.4 5.1 reshape.135
  344.5 25.6 %all_to_all.131 = bf16[4,2,51200]{2,1,0:T(2,128)(2,1)} all-to-all(bf16[4,2,51200]{2,1,0:T(2,128)(2,1)} %reshape.135), channel_id=1, replica_groups=mesh['rep'=8,'tp'=4] {'tp'}, dimensions={0} | all-to-all | bytes 1638400 | tf_op jit(solution)/shard_map/all_to_all | solution.py:54
  370.2 5.0 reshape.136
  392.4 8.8 fusion.26
  401.2 29.3 %all-gather.21.cloned.1.call-done = bf16[2,1280,1280]{2,1,0:T(8,128)(2,1)} async-done(((bf16[2,160,1280]{2,1,0:T(8,128)(2,1)}), bf16[2,1280,1280]{2,1,0:T(8,128)(2,1)}) %all-gather.21.cloned.1.call-update) | async-done | bytes 6553616 | tf_op jit(solution)/shard_map/all_gather | solution.py:62
  430.5 48.4 %all-gather.23.cloned.1.call-done = bf16[2,1280,1280]{2,1,0:T(8,128)(2,1)} async-done(((bf16[2,160,1280]{2,1,0:T(8,128)(2,1)}), bf16[2,1280,1280]{2,1,0:T(8,128)(2,1)}) %all-gather.23.cloned.1.call-update) | async-done | bytes 6553616 | tf_op jit(solution)/shard_map/all_gather | solution.py:63
  478.9 23.3 %convolution_convert_fusion.2 = bf16[1024,1280]{1,0:T(8,128)(2,1)} fusion(bf16[2,1280,1280]{2,1,0:T(8,128)(2,1)} %all-gather.23.cloned.1.call-done, f32[1024,1280]{1,0:T(8,128)} %fusion.26, bf16[1024,1280]{1,0:T(8,128)(2,1)} %multiply_convert_fusion.2, bf16[2,1280,1280]{2,1,0:T(8,128)(2,1)} %all-gather.21.cloned.1.call-done), kind=kOutput, calls=%fused_computation.57 | convolution fusion | flops 6798704640 | bytes 17039360 | tf_op jit(solution)/shard_map/dot_general | solution.py:88
  502.3 104.2 %all-reduce.7.cloned.1.call-done = bf16[1024,1280]{1,0:T(8,128)(2,1)} async-done(((bf16[1024,1280]{1,0:T(8,128)(2,1)}), bf16[1024,1280]{1,0:T(8,128)(2,1)}) %all-reduce.7.cloned.1.call-update) | async-done | bytes 2621456 | tf_op jit(solution)/shard_map/psum | solution.py:124
  637.8 103.2 %all-reduce.9.cloned.1.call-done = bf16[1024,1280]{1,0:T(8,128)(2,1)} async-done(((bf16[1024,1280]{1,0:T(8,128)(2,1)}), bf16[1024,1280]{1,0:T(8,128)(2,1)}) %all-reduce.9.cloned.1.call-update) | async-done | bytes 2621456 | tf_op jit(solution)/shard_map/psum | solution.py:124
  747.2 7.9 fusion.25
  755.1 24.4 %convolution_convert_fusion = bf16[1024,1280]{1,0:T(8,128)(2,1)} fusion(bf16[2,1280,1280]{2,1,0:T(8,128)(2,1)} %all-gather.23.cloned.1.call-done, f32[1024,1280]{1,0:T(8,128)} %fusion.25, bf16[2,1280,1280]{2,1,0:T(8,128)(2,1)} %all-gather.21.cloned.1.call-done, f32[1024,1280]{1,0:T(8,128)} %copy-done.5, f32[1280]{0:T(1024)S(1)} %get-tuple-element.5, ...), kind=kOutput, calls=%fused_computation.55 | convolution fusion | flops 6803947520 | bytes 19674112 | tf_op jit(solution)/shard_map/dot_general | solution.py:88
  779.4 103.2 %all-reduce.11.cloned.1.call-done = bf16[1024,1280]{1,0:T(8,128)(2,1)} async-done(((bf16[1024,1280]{1,0:T(8,128)(2,1)}), bf16[1024,1280]{1,0:T(8,128)(2,1)}) %all-reduce.11.cloned.1.call-update) | async-done | bytes 2621456 | tf_op jit(solution)/shard_map/psum | solution.py:124
  (138 shorter events, 116.2 us)
Async XLA Ops:
  6.5 85.3 %copy-start = (f32[32,1280]{1,0:T(8,128)S(1)}, f32[32,1280]{1,0:T(8,128)}, u32[]{:S(2)}) copy-start(f32[32,1280]{1,0:T(8,128)} %param.16) | copy-start | bytes 491524
  6.5 19.6 %copy-start.6 = (bf16[2,40,1280]{2,1,0:T(8,128)(2,1)S(1)}, bf16[2,40,1280]{2,1,0:T(8,128)(2,1)}, u32[]{:S(2)}) copy-start(bf16[2,40,1280]{2,1,0:T(8,128)(2,1)} %param.20) | copy-start | bytes 614404
  6.5 43.5 %copy-start.7 = (bf16[2,40,1280]{2,1,0:T(8,128)(2,1)S(1)}, bf16[2,40,1280]{2,1,0:T(8,128)(2,1)}, u32[]{:S(2)}) copy-start(bf16[2,40,1280]{2,1,0:T(8,128)(2,1)} %param.21) | copy-start | bytes 614404
  6.5 85.3 %all-gather.9.cloned.1.call-start = ((), (), s32[]{:S(2)}) async-start(), calls=%async_computation.7 | async-start | bytes 3276800 | tf_op jit(solution)/shard_map/all_gather | solution.py:117
  7.3 97.5 %all-gather.13.cloned.1.call-start = ((), (), s32[]{:S(2)}) async-start(), calls=%async_computation.9 | async-start | bytes 2211840 | tf_op jit(solution)/shard_map/all_gather | solution.py:57
  24.6 44.4 %copy-start.8 = (bf16[2,40,1280]{2,1,0:T(8,128)(2,1)S(1)}, bf16[2,40,1280]{2,1,0:T(8,128)(2,1)}, u32[]{:S(2)}) copy-start(bf16[2,40,1280]{2,1,0:T(8,128)(2,1)} %param.22) | copy-start | bytes 614404
  26.1 107.8 %all-gather.15.cloned.1.call-start = ((), (), s32[]{:S(2)}) async-start(), calls=%async_computation.10 | async-start | bytes 2211840 | tf_op jit(solution)/shard_map/all_gather | solution.py:58
  26.7 48.7 %copy-start.12 = (s32[4]{0:T(128)S(1)}, s32[4]{0:T(128)}, u32[]{:S(2)}) copy-start(s32[4]{0:T(128)} %param.15) | copy-start | bytes 52
  26.7 48.8 %copy-start.11 = (s32[4,4]{1,0:T(4,128)S(1)}, s32[4,4]{1,0:T(4,128)}, u32[]{:S(2)}) copy-start(s32[4,4]{1,0:T(4,128)} %param.14) | copy-start | bytes 196
  26.7 48.9 %copy-start.9 = (f32[2,1280]{1,0:T(2,128)S(1)}, f32[2,1280]{1,0:T(2,128)}, u32[]{:S(2)}) copy-start(f32[2,1280]{1,0:T(2,128)} %param.17) | copy-start | bytes 30724
  50.0 112.9 %all-gather.11.cloned.1.call-start = ((), (), s32[]{:S(2)}) async-start(), calls=%async_computation.8 | async-start | bytes 2211840 | tf_op jit(solution)/shard_map/all_gather | solution.py:59
  71.3 15.0 %all-to-all-start.3 = ((bf16[4,2,12800]{2,1,0:T(2,128)(2,1)}), bf16[4,2,12800]{2,1,0:T(2,128)(2,1)}, u32[]{:S(2)}, u32[]{:S(2)}) async-start(bf16[4,2,12800]{2,1,0:T(2,128)(2,1)} %reshape.143), calls=%async_computation.3 | async-start | bytes 409600 | tf_op jit(solution)/shard_map/all_to_all | solution.py:51
  75.3 116.7 %all-gather.17.cloned.1.call-start = ((), (), s32[]{:S(2)}) async-start(), calls=%async_computation.11 | async-start | bytes 2211840 | tf_op jit(solution)/shard_map/all_gather | solution.py:60
  91.6 290.2 %all-reduce.5.cloned.1.call-start = ((), (), s32[]{:S(2)}) async-start(), calls=%async_computation.12 | async-start | bytes 5242880 | tf_op jit(solution)/shard_map/psum | solution.py:124
  97.0 2.3 copy-start.2
  196.3 196.1 %all-gather.19.cloned.1.call-start = ((), (), s32[]{:S(2)}) async-start(), calls=%async_computation.13 | async-start | bytes 7372800 | tf_op jit(solution)/shard_map/all_gather | solution.py:61
  265.8 164.7 %all-gather.21.cloned.1.call-start = ((), (), s32[]{:S(2)}) async-start(), calls=%async_computation.14 | async-start | bytes 7372800 | tf_op jit(solution)/shard_map/all_gather | solution.py:62
  334.7 144.3 %all-gather.23.cloned.1.call-start = ((), (), s32[]{:S(2)}) async-start(), calls=%async_computation.15 | async-start | bytes 7372800 | tf_op jit(solution)/shard_map/all_gather | solution.py:63
  344.5 37.2 %copy-start.10 = (f32[2,1280]{1,0:T(2,128)S(1)}, f32[2,1280]{1,0:T(2,128)}, u32[]{:S(2)}) copy-start(f32[2,1280]{1,0:T(2,128)} %param.18) | copy-start | bytes 30724
  381.6 224.9 %all-reduce.7.cloned.1.call-start = ((), (), s32[]{:S(2)}) async-start(), calls=%async_computation.16 | async-start | bytes 5242880 | tf_op jit(solution)/shard_map/psum | solution.py:124
  381.8 4.1 copy-start.4
  381.8 7.7 slice-start
  385.8 3.7 slice-start.1
  502.3 238.7 %all-reduce.9.cloned.1.call-start = ((), (), s32[]{:S(2)}) async-start(), calls=%async_computation.17 | async-start | bytes 5242880 | tf_op jit(solution)/shard_map/psum | solution.py:124
  610.7 2.3 copy-start.3
  611.4 2.7 copy-start.13
  631.8 2.7 copy-start.14
  637.8 244.9 %all-reduce.11.cloned.1.call-start = ((), (), s32[]{:S(2)}) async-start(), calls=%async_computation.18 | async-start | bytes 5242880 | tf_op jit(solution)/shard_map/psum | solution.py:124
  744.9 2.3 copy-start.5
  755.0 130.1 %copy-start.1 = (f32[32,1280]{1,0:T(8,128)S(1)}, f32[32,1280]{1,0:T(8,128)}, u32[]{:S(2)}) copy-start(f32[32,1280]{1,0:T(8,128)} %param.16) | copy-start | bytes 491524
Sparse Core Ops, SparseCore 0:
  8.9 66.1 all-gather.8
  77.0 27.7 all-gather.12
  106.7 27.2 all-gather.14
  135.7 27.2 all-gather.10
  164.7 27.2 all-gather.16
  196.4 138.2 all-reduce.4
  336.6 45.3 all-gather.18
  384.0 46.4 all-gather.20
  432.4 46.4 all-gather.22
  502.4 104.0 all-reduce.6
  637.9 103.0 all-reduce.8
  779.6 103.0 all-reduce.10
where the time goes:
time: 902 us; the launch traced here: 892 us
  waiting for transfers between devices  460 us (51%)
  blocking collectives  169 us (19%)
  matrix products  105 us (12%)
  local copies, waits for them, and re-layouts  103 us (11%)
  other arithmetic  35.2 us (4%)
  between operations  14.7 us (2%)
    psum x4, waiting for transfers between devices, total_terms(): lax.psum(partial_value.astype(jnp.bfloat16), 'tp').astype(jnp.float32)  311 us
    unnamed x57, local copies, waits for them, and re-layouts  62.7 us
    dot_general x4, matrix products, out_terms(): lax.dot_general(mixed_rows, weight, (((1,), (1,)), ((), ())), preferred_e...  55.2 us
    all_gather x1, waiting for transfers between devices, reshard(): lax.all_gather(owned[6], 'rep', axis=1, tiled=True)  48.4 us
    all_to_all x1, blocking collectives, reshard(): lax.all_to_all(weights[4], 'tp', split_axis=2, concat_axis=1, tiled=True)  47.9 us
    all_to_all x1, blocking collectives, reshard(): lax.all_to_all(weights[5], 'tp', split_axis=2, concat_axis=1, tiled=True)  47.5 us
    all_gather x1, waiting for transfers between devices, reshard(): lax.all_gather(owned[5], 'rep', axis=1, tiled=True)  29.3 us
    all_to_all x1, blocking collectives, reshard(): lax.all_to_all(weights[6], 'tp', split_axis=2, concat_axis=1, tiled=True)  25.6 us
  transfers between devices with their start and end apart: 13, of which 9 were waited for; matrix products, arithmetic and copies ran while one was open for 16% of the time, Pallas kernels for 0%

commit v1 on v0

--- a/solution.py
+++ b/solution.py
@@ -60,7 +60,7 @@
         lax.all_gather(owned[3], "rep", axis=1, tiled=True),
         lax.all_gather(owned[4], "rep", axis=1, tiled=True),
         lax.all_gather(owned[5], "rep", axis=1, tiled=True),
-        lax.all_gather(owned[6], "rep", axis=1, tiled=True),
+        jnp.concatenate(lax.all_gather(owned[6], "rep"), axis=1),
     )
 
 

time: 902 us -> 899 us (level)
    all_to_all x1, blocking collectives: 25.6 us -> 47.5 us  [reshard(): lax.all_to_all(weights[6], 'tp', split_axis=2, concat_axis=1, tiled=True)]
    all_to_all x1, blocking collectives: 47.5 us -> 25.7 us  [reshard(): lax.all_to_all(weights[5], 'tp', split_axis=2, concat_axis=1, tiled=True)]
    all_gather x1, waiting for transfers between devices: 48.4 us -> 29.4 us  [reshard(): lax.all_gather(owned[6], 'rep')]
    all_gather x1, waiting for transfers between devices: 29.3 us -> 42.4 us  [reshard(): lax.all_gather(owned[5], 'rep', axis=1, tiled=True)]
    unnamed x57 -> x59, local copies, waits for them, and re-layouts: 62.7 us -> 61.2 us
  transfers between devices with their start and end apart: 13 -> 13, of which waited for: 9 -> 9; matrix products, arithmetic and copies ran while one was open for 16% -> 17% of each run, Pallas kernels for 0% -> 0%
where the time goes in v1:
time: 899 us; the launch traced here: 889 us
  waiting for transfers between devices  454 us (51%)
  blocking collectives  169 us (19%)
  local copies, waits for them, and re-layouts  108 us (12%)
  matrix products  103 us (11%)
  other arithmetic  35 us (4%)
  between operations  14.4 us (2%)
    psum x4, waiting for transfers between devices, total_terms(): lax.psum(partial_value.astype(jnp.bfloat16), 'tp').astype(jnp.float32)  311 us
    unnamed x59, local copies, waits for them, and re-layouts  61.2 us
    dot_general x4, matrix products, out_terms(): lax.dot_general(mixed_rows, weight, (((1,), (1,)), ((), ())), preferred_e...  52.3 us
    all_to_all x1, blocking collectives, reshard(): lax.all_to_all(weights[4], 'tp', split_axis=2, concat_axis=1, tiled=True)  47.9 us
    all_to_all x1, blocking collectives, reshard(): lax.all_to_all(weights[6], 'tp', split_axis=2, concat_axis=1, tiled=True)  47.5 us
    all_gather x1, waiting for transfers between devices, reshard(): lax.all_gather(owned[5], 'rep', axis=1, tiled=True)  42.4 us
    all_gather x1, waiting for transfers between devices, reshard(): lax.all_gather(owned[6], 'rep')  29.4 us
    all_to_all x1, blocking collectives, reshard(): lax.all_to_all(weights[5], 'tp', split_axis=2, concat_axis=1, tiled=True)  25.7 us
  transfers between devices with their start and end apart: 13, of which 9 were waited for; matrix products, arithmetic and copies ran while one was open for 17% of the time, Pallas kernels for 0%

profile of v1, /device:TPU:0, one launch (start us, length us, event | category | flops | bytes accessed | tf_op | source)
XLA Modules:
  0.0 889.0 jit_solution(12029725930016066722)
XLA Ops:
  9.8 13.8 %all_to_all.123 = bf16[4,2,12800]{2,1,0:T(2,128)(2,1)S(1)} all-to-all(bf16[4,2,12800]{2,1,0:T(2,128)(2,1)S(1)} %reshape.149), channel_id=1, replica_groups=mesh['rep'=8,'tp'=4] {'tp'}, dimensions={0} | all-to-all | bytes 409600 | tf_op jit(solution)/shard_map/all_to_all | solution.py:48
  27.8 19.7 %all_to_all.124 = bf16[4,2,12800]{2,1,0:T(2,128)(2,1)S(1)} all-to-all(bf16[4,2,12800]{2,1,0:T(2,128)(2,1)S(1)} %reshape.147), channel_id=1, replica_groups=mesh['rep'=8,'tp'=4] {'tp'}, dimensions={0} | all-to-all | bytes 409600 | tf_op jit(solution)/shard_map/all_to_all | solution.py:49
  51.7 14.8 %all_to_all.125 = bf16[4,2,12800]{2,1,0:T(2,128)(2,1)S(1)} all-to-all(bf16[4,2,12800]{2,1,0:T(2,128)(2,1)S(1)} %reshape.151), channel_id=1, replica_groups=mesh['rep'=8,'tp'=4] {'tp'}, dimensions={0} | all-to-all | bytes 409600 | tf_op jit(solution)/shard_map/all_to_all | solution.py:50
  75.7 10.5 %multiply_cosine_fusion = (f32[1024,640]{1,0:T(8,128)S(1)}, f32[1024,640]{1,0:T(8,128)}) fusion(f32[640]{0:T(1024)S(1)} %multiply_exponential_fusion, f32[1024]{0:T(1024)S(1)} %convert_element_type.93), kind=kLoop, calls=%fused_computation.60 | loop fusion | flops 655360 | bytes 5249536 | tf_op jit(solution)/shard_map/cos | solution.py:25
  92.1 5.1 fusion.140
  100.2 4.6 all-gather.13.cloned.1.call-done
  109.7 24.3 %all-gather.15.cloned.1.call-done = bf16[2,1280,320]{2,1,0:T(8,128)(2,1)} async-done(((bf16[2,160,320]{2,1,0:T(8,128)(2,1)}), bf16[2,1280,320]{2,1,0:T(8,128)(2,1)}) %all-gather.15.cloned.1.call-update) | async-done | bytes 1638416 | tf_op jit(solution)/shard_map/all_gather | solution.py:58
  139.6 23.4 %all-gather.11.cloned.1.call-done = bf16[2,1280,320]{2,1,0:T(8,128)(2,1)} async-done(((bf16[2,160,320]{2,1,0:T(8,128)(2,1)}), bf16[2,1280,320]{2,1,0:T(8,128)(2,1)}) %all-gather.11.cloned.1.call-update) | async-done | bytes 1638416 | tf_op jit(solution)/shard_map/all_gather | solution.py:59
  173.8 18.1 %all-gather.17.cloned.1.call-done = bf16[2,1280,320]{2,1,0:T(8,128)(2,1)} async-done(((bf16[2,160,320]{2,1,0:T(8,128)(2,1)}), bf16[2,1280,320]{2,1,0:T(8,128)(2,1)}) %all-gather.17.cloned.1.call-update) | async-done | bytes 1638416 | tf_op jit(solution)/shard_map/all_gather | solution.py:60
  192.0 4.3 convolution_convert_fusion.3
  196.6 4.7 copy.97
  201.3 5.1 reshape.155
  206.3 47.9 %all_to_all.126 = bf16[4,2,51200]{2,1,0:T(2,128)(2,1)} all-to-all(bf16[4,2,51200]{2,1,0:T(2,128)(2,1)} %reshape.155), channel_id=1, replica_groups=mesh['rep'=8,'tp'=4] {'tp'}, dimensions={0} | all-to-all | bytes 1638400 | tf_op jit(solution)/shard_map/all_to_all | solution.py:52
  254.2 5.0 reshape.156
  265.8 4.7 copy.103
  270.5 5.1 reshape.145
  275.6 47.5 %all_to_all.127 = bf16[4,2,51200]{2,1,0:T(2,128)(2,1)} all-to-all(bf16[4,2,51200]{2,1,0:T(2,128)(2,1)} %reshape.145), channel_id=1, replica_groups=mesh['rep'=8,'tp'=4] {'tp'}, dimensions={0} | all-to-all | bytes 1638400 | tf_op jit(solution)/shard_map/all_to_all | solution.py:54
  323.2 5.0 reshape.146
  334.8 4.7 copy.100
  339.5 5.1 reshape.157
  344.6 25.7 %all_to_all.128 = bf16[4,2,51200]{2,1,0:T(2,128)(2,1)} all-to-all(bf16[4,2,51200]{2,1,0:T(2,128)(2,1)} %reshape.157), channel_id=1, replica_groups=mesh['rep'=8,'tp'=4] {'tp'}, dimensions={0} | all-to-all | bytes 1638400 | tf_op jit(solution)/shard_map/all_to_all | solution.py:53
  370.2 5.0 reshape.158
  392.3 8.8 fusion.26
  401.2 29.4 %all-gather.23.cloned.1.call-done = bf16[8,2,160,1280]{3,2,1,0:T(8,128)(2,1)} async-done(((bf16[1,2,160,1280]{3,2,1,0:T(8,128)(2,1)}), bf16[8,2,160,1280]{3,2,1,0:T(8,128)(2,1)}) %all-gather.23.cloned.1.call-update) | async-done | bytes 6553616 | tf_op jit(solution)/shard_map/all_gather | solution.py:63
  430.5 6.0 fusion.139
  436.6 42.4 %all-gather.21.cloned.1.call-done = bf16[2,1280,1280]{2,1,0:T(8,128)(2,1)} async-done(((bf16[2,160,1280]{2,1,0:T(8,128)(2,1)}), bf16[2,1280,1280]{2,1,0:T(8,128)(2,1)}) %all-gather.21.cloned.1.call-update) | async-done | bytes 6553616 | tf_op jit(solution)/shard_map/all_gather | solution.py:62
  479.0 23.6 %convolution_convert_fusion.2 = bf16[1024,1280]{1,0:T(8,128)(2,1)} fusion(bf16[1280,1280]{1,0:T(8,128)(2,1)} %bitcast.127, f32[1024,1280]{1,0:T(8,128)} %fusion.26, bf16[1024,1280]{1,0:T(8,128)(2,1)} %multiply_convert_fusion.2, bf16[2,1280,1280]{2,1,0:T(8,128)(2,1)} %all-gather.21.cloned.1.call-done), kind=kOutput, calls=%fused_computation.57 | convolution fusion | flops 6798704640 | bytes 17039360 | tf_op jit(solution)/shard_map/dot_general | solution.py:88
  502.6 104.2 %all-reduce.7.cloned.1.call-done = bf16[1024,1280]{1,0:T(8,128)(2,1)} async-done(((bf16[1024,1280]{1,0:T(8,128)(2,1)}), bf16[1024,1280]{1,0:T(8,128)(2,1)}) %all-reduce.7.cloned.1.call-update) | async-done | bytes 2621456 | tf_op jit(solution)/shard_map/psum | solution.py:124
  638.0 103.2 %all-reduce.9.cloned.1.call-done = bf16[1024,1280]{1,0:T(8,128)(2,1)} async-done(((bf16[1024,1280]{1,0:T(8,128)(2,1)}), bf16[1024,1280]{1,0:T(8,128)(2,1)}) %all-reduce.9.cloned.1.call-update) | async-done | bytes 2621456 | tf_op jit(solution)/shard_map/psum | solution.py:124
  745.8 9.1 %fusion.25 = f32[1024,1280]{1,0:T(8,128)} fusion(bf16[2,1280,1280]{2,1,0:T(8,128)(2,1)} %all-gather.19.cloned.1.call-done, f32[1024,1280]{1,0:T(8,128)S(1)} %get-tuple-element.10, f32[1280]{0:T(1024)S(1)} %get-tuple-element.5, f32[1024]{0:T(1024)S(1)} %add_rsqrt_fusion, f32[1024]{0:T(1024)S(1)} %broadcast_multiply_fusion), kind=kOutput, calls=%fused_computation.63 | convolution fusion | flops 3360686080 | bytes 13775872 | tf_op jit(solution)/shard_map/dot_general | solution.py:148
  754.9 21.3 %convolution_convert_fusion = bf16[1024,1280]{1,0:T(8,128)(2,1)} fusion(bf16[1280,1280]{1,0:T(8,128)(2,1)S(1)} %bitcast.126, f32[1024,1280]{1,0:T(8,128)} %fusion.25, bf16[2,1280,1280]{2,1,0:T(8,128)(2,1)} %all-gather.21.cloned.1.call-done, f32[1024,1280]{1,0:T(8,128)} %copy-done.5, f32[1280]{0:T(1024)S(1)} %get-tuple-element.5, ...), kind=kOutput, calls=%fused_computation.55 | convolution fusion | flops 6803947520 | bytes 19674112 | tf_op jit(solution)/shard_map/dot_general | solution.py:88
  776.2 103.2 %all-reduce.11.cloned.1.call-done = bf16[1024,1280]{1,0:T(8,128)(2,1)} async-done(((bf16[1024,1280]{1,0:T(8,128)(2,1)}), bf16[1024,1280]{1,0:T(8,128)(2,1)}) %all-reduce.11.cloned.1.call-update) | async-done | bytes 2621456 | tf_op jit(solution)/shard_map/psum | solution.py:124
  (141 shorter events, 119.0 us)
Async XLA Ops:
  6.5 85.6 %copy-start = (f32[32,1280]{1,0:T(8,128)S(1)}, f32[32,1280]{1,0:T(8,128)}, u32[]{:S(2)}) copy-start(f32[32,1280]{1,0:T(8,128)} %param.16) | copy-start | bytes 491524
  6.5 19.6 %copy-start.7 = (bf16[2,40,1280]{2,1,0:T(8,128)(2,1)S(1)}, bf16[2,40,1280]{2,1,0:T(8,128)(2,1)}, u32[]{:S(2)}) copy-start(bf16[2,40,1280]{2,1,0:T(8,128)(2,1)} %param.20) | copy-start | bytes 614404
  6.5 43.5 %copy-start.8 = (bf16[2,40,1280]{2,1,0:T(8,128)(2,1)S(1)}, bf16[2,40,1280]{2,1,0:T(8,128)(2,1)}, u32[]{:S(2)}) copy-start(bf16[2,40,1280]{2,1,0:T(8,128)(2,1)} %param.21) | copy-start | bytes 614404
  6.5 85.5 %all-gather.9.cloned.1.call-start = ((), (), s32[]{:S(2)}) async-start(), calls=%async_computation.7 | async-start | bytes 3276800 | tf_op jit(solution)/shard_map/all_gather | solution.py:117
  7.3 97.5 %all-gather.13.cloned.1.call-start = ((), (), s32[]{:S(2)}) async-start(), calls=%async_computation.9 | async-start | bytes 2211840 | tf_op jit(solution)/shard_map/all_gather | solution.py:57
  24.6 44.4 %copy-start.9 = (bf16[2,40,1280]{2,1,0:T(8,128)(2,1)S(1)}, bf16[2,40,1280]{2,1,0:T(8,128)(2,1)}, u32[]{:S(2)}) copy-start(bf16[2,40,1280]{2,1,0:T(8,128)(2,1)} %param.22) | copy-start | bytes 614404
  26.1 107.9 %all-gather.15.cloned.1.call-start = ((), (), s32[]{:S(2)}) async-start(), calls=%async_computation.10 | async-start | bytes 2211840 | tf_op jit(solution)/shard_map/all_gather | solution.py:58
  26.7 48.7 %copy-start.13 = (s32[4]{0:T(128)S(1)}, s32[4]{0:T(128)}, u32[]{:S(2)}) copy-start(s32[4]{0:T(128)} %param.15) | copy-start | bytes 52
  26.7 48.8 %copy-start.12 = (s32[4,4]{1,0:T(4,128)S(1)}, s32[4,4]{1,0:T(4,128)}, u32[]{:S(2)}) copy-start(s32[4,4]{1,0:T(4,128)} %param.14) | copy-start | bytes 196
  26.7 48.9 %copy-start.10 = (f32[2,1280]{1,0:T(2,128)S(1)}, f32[2,1280]{1,0:T(2,128)}, u32[]{:S(2)}) copy-start(f32[2,1280]{1,0:T(2,128)} %param.17) | copy-start | bytes 30724
  50.0 113.0 %all-gather.11.cloned.1.call-start = ((), (), s32[]{:S(2)}) async-start(), calls=%async_computation.8 | async-start | bytes 2211840 | tf_op jit(solution)/shard_map/all_gather | solution.py:59
  71.3 14.9 %all-to-all-start.3 = ((bf16[4,2,12800]{2,1,0:T(2,128)(2,1)}), bf16[4,2,12800]{2,1,0:T(2,128)(2,1)}, u32[]{:S(2)}, u32[]{:S(2)}) async-start(bf16[4,2,12800]{2,1,0:T(2,128)(2,1)} %reshape.153), calls=%async_computation.3 | async-start | bytes 409600 | tf_op jit(solution)/shard_map/all_to_all | solution.py:51
  75.3 116.7 %all-gather.17.cloned.1.call-start = ((), (), s32[]{:S(2)}) async-start(), calls=%async_computation.11 | async-start | bytes 2211840 | tf_op jit(solution)/shard_map/all_gather | solution.py:60
  91.6 290.3 %all-reduce.5.cloned.1.call-start = ((), (), s32[]{:S(2)}) async-start(), calls=%async_computation.12 | async-start | bytes 5242880 | tf_op jit(solution)/shard_map/psum | solution.py:124
  97.2 2.3 copy-start.2
  196.3 196.0 %all-gather.19.cloned.1.call-start = ((), (), s32[]{:S(2)}) async-start(), calls=%async_computation.13 | async-start | bytes 7372800 | tf_op jit(solution)/shard_map/all_gather | solution.py:61
  265.7 164.8 %all-gather.23.cloned.1.call-start = ((), (), s32[]{:S(2)}) async-start(), calls=%async_computation.15 | async-start | bytes 7372800 | tf_op jit(solution)/shard_map/all_gather | solution.py:63
  334.7 144.3 %all-gather.21.cloned.1.call-start = ((), (), s32[]{:S(2)}) async-start(), calls=%async_computation.14 | async-start | bytes 7372800 | tf_op jit(solution)/shard_map/all_gather | solution.py:62
  344.6 37.2 %copy-start.11 = (f32[2,1280]{1,0:T(2,128)S(1)}, f32[2,1280]{1,0:T(2,128)}, u32[]{:S(2)}) copy-start(f32[2,1280]{1,0:T(2,128)} %param.18) | copy-start | bytes 30724
  381.8 225.0 %all-reduce.7.cloned.1.call-start = ((), (), s32[]{:S(2)}) async-start(), calls=%async_computation.16 | async-start | bytes 5242880 | tf_op jit(solution)/shard_map/psum | solution.py:124
  381.9 4.1 copy-start.4
  381.9 7.7 slice-start
  386.0 3.7 slice-start.1
  502.6 238.6 %all-reduce.9.cloned.1.call-start = ((), (), s32[]{:S(2)}) async-start(), calls=%async_computation.17 | async-start | bytes 5242880 | tf_op jit(solution)/shard_map/psum | solution.py:124
  611.0 2.3 copy-start.3
  611.7 2.7 copy-start.14
  632.0 2.7 copy-start.15
  637.9 241.6 %all-reduce.11.cloned.1.call-start = ((), (), s32[]{:S(2)}) async-start(), calls=%async_computation.18 | async-start | bytes 5242880 | tf_op jit(solution)/shard_map/psum | solution.py:124
  745.1 9.8 %copy-start.5 = (f32[1024,1280]{1,0:T(8,128)}, f32[1024,1280]{1,0:T(8,128)S(1)}, u32[]{:S(2)}) copy-start(f32[1024,1280]{1,0:T(8,128)S(1)} %get-tuple-element.10) | copy-start | bytes 15728644
  745.8 9.1 %copy-start.6 = (bf16[1,8,160,1280]{3,2,0,1:T(8,128)(2,1)S(1)}, bf16[1,8,160,1280]{3,2,0,1:T(8,128)(2,1)}, u32[]{:S(2)}) copy-start(bf16[1,8,160,1280]{3,2,0,1:T(8,128)(2,1)} %get-tuple-element.13) | copy-start | bytes 9830404
  754.9 127.0 %copy-start.1 = (f32[32,1280]{1,0:T(8,128)S(1)}, f32[32,1280]{1,0:T(8,128)}, u32[]{:S(2)}) copy-start(f32[32,1280]{1,0:T(8,128)} %param.16) | copy-start | bytes 491524
Sparse Core Ops, SparseCore 0:
  8.9 66.1 all-gather.8
  77.0 27.7 all-gather.12
  106.7 27.2 all-gather.14
  135.7 27.2 all-gather.10
  164.7 27.2 all-gather.16
  196.4 138.2 all-reduce.4
  336.7 45.3 all-gather.18
  384.0 46.4 all-gather.22
  432.4 46.4 all-gather.20
  502.7 104.0 all-reduce.6
  638.0 103.0 all-reduce.8
  776.4 103.0 all-reduce.10
